TPU v7x, 32 devices: a whole 2x2x4 slice. The times are simulated.
32 devices in a mesh: blk: 4 (over z), team: 4 (over y, core), heads: 2 (over x).
Axes of the slice: x: 2, y: 2, z: 4, core: 2. Of those that a mesh axis runs over, the one named last changes fastest.
Arguments:
- queries: bfloat16 [512, 1024], P('blk', ('team', 'heads')), may hold values from -16 to 16
- keys: bfloat16 [512, 256], P(('blk', 'team'), 'heads'), may hold values from -16 to 16
- values: bfloat16 [512, 256], P(('blk', 'team'), 'heads'), may hold values from -6 to 6
- out_grads: bfloat16 [512, 1024], P('blk', ('team', 'heads')), may hold values from -6 to 6
- positions: int32 [512], P('blk'), may hold values from 0 to 511, as said below
Outputs:
- query_grad: bfloat16 [512, 1024], P('blk', ('team', 'heads'))
- key_grad: bfloat16 [512, 256], P(('blk', 'team'), 'heads')
- value_grad: bfloat16 [512, 256], P(('blk', 'team'), 'heads')
Inputs may be any that keep to these rules, and one draw needn't show every extreme that they name: positions hold every number of 0 to 511 once; every aligned run of 32 rows holds 32 consecutive rising positions.
All inputs are finite; a program needn't handle non-finite values.
Results may differ from a plain program's by a relative error of at most 0.0069.
Values may be sent and summed in bfloat16 or wider, within the bound.
A program may use at most 64 MiB of HBM per device.

v0:
```python
import functools
import math

import jax
import jax.numpy as jnp
from jax import lax
from jax.experimental import pallas as pl
from jax.experimental.pallas import tpu as pltpu
from jax.sharding import PartitionSpec as P

masked_score = -1e30
MESH = pl.DeviceIdType.MESH


def contract_last(left, right):
    return lax.dot_general(
        left, right, (((1,), (1,)), ((), ())), preferred_element_type=jnp.float32
    )


def contract_first(left, right):
    return lax.dot_general(
        left, right, (((0,), (0,)), ((), ())), preferred_element_type=jnp.float32
    )


def each(count, body):
    if count <= 16:
        for index in range(count):
            body(index)
    else:

        def step(index, carry):
            body(index)
            return carry

        lax.fori_loop(0, count, step, 0)


def join_rows(pieces):
    count, rows, width = pieces.shape
    if rows % 16:
        return pieces.astype(jnp.float32).reshape(count * rows, width).astype(pieces.dtype)
    return pieces.reshape(count * rows, width)


def near_first(index, blocks):
    if index == 0:
        return 0
    return (index + 1) // 2 if index % 2 else blocks - index // 2


def kernel(
    blocks,
    team,
    q_hbm,
    k_hbm,
    v_hbm,
    g_hbm,
    p_hbm,
    qg_ref,
    kg_ref,
    vg_ref,
    q_ref,
    g_ref,
    p_ref,
    kv,
    places,
    scores,
    products,
    slopes_ref,
    columns,
    tops,
    parts,
    staged,
    sums_ref,
    landed,
    load_sem,
    own_send,
    own_recv,
    pass_send,
    pass_recv,
    place_send,
    place_recv,
    stage_send,
    stage_recv,
    part_send,
    part_recv,
):
    my_blk, my_team = lax.axis_index("blk"), lax.axis_index("team")
    me = my_blk * team + my_team
    rows, head_dim = q_ref.shape
    piece = k_hbm.shape[0]
    scale = 1.0 / math.sqrt(head_dim)
    half = team // 2
    side = lax.rem(my_team, 2)
    my_half = lax.div(my_team, 2)
    twin = my_team + 1 - 2 * side

    def half_at(distance):
        return lax.rem(my_half + distance, half)

    def block_at(distance):
        return lax.rem(my_blk + distance, blocks)

    def mate_at(distance):
        return lax.rem(my_team + distance, team)

    def blk_peer(blk_now):
        return {"blk": blk_now, "team": my_team}

    def team_peer(team_now):
        return {"blk": my_blk, "team": team_now}

    def send(src, dst, send_sem, recv_sem, peer):
        pltpu.make_async_remote_copy(
            src_ref=src,
            dst_ref=dst,
            send_sem=send_sem,
            recv_sem=recv_sem,
            device_id=peer,
            device_id_type=MESH,
        ).start()

    def wait_bytes(ref, sem):
        pltpu.make_async_copy(ref, ref, sem).wait()

    barrier = pltpu.get_barrier_semaphore()

    def greet(peer):
        pl.semaphore_signal(barrier, inc=1, device_id=peer, device_id_type=MESH)

    def greet_side(index):
        away = jnp.int32(blocks * half - 1 - index)
        blk_now = block_at(lax.div(away, jnp.int32(half)))
        greet({"blk": blk_now, "team": 2 * half_at(lax.rem(away, jnp.int32(half))) + side})

    each(blocks * half - 1, greet_side)
    each(half, lambda i: greet(team_peer(2 * i + 1 - side)))

    loads = [
        pltpu.make_async_copy(p_hbm, p_ref, load_sem.at[0]),
        pltpu.make_async_copy(k_hbm, kv.at[me, 0], load_sem.at[1]),
        pltpu.make_async_copy(v_hbm, kv.at[me, 1], load_sem.at[2]),
        pltpu.make_async_copy(q_hbm, q_ref, load_sem.at[3]),
        pltpu.make_async_copy(g_hbm, g_ref, load_sem.at[4]),
    ]
    for which in (1, 2, 0, 3, 4):
        loads[which].start()

    loads[0].wait()
    place_row = p_ref[...].astype(jnp.float32)
    places[my_blk] = place_row
    loads[1].wait()
    loads[2].wait()
    pl.semaphore_wait(barrier, blocks * half - 1 + half)

    def send_far(index):
        blk_now = block_at(blocks - 1 - index)
        send(kv.at[me], kv.at[me], own_send, own_recv.at[my_blk], blk_peer(blk_now))

    def send_places(index):
        blk_now = block_at(index + 1)
        send(places.at[my_blk], places.at[my_blk], place_send, place_recv, blk_peer(blk_now))

    def pass_on(blk_now):
        slot = kv.at[blk_now * team + my_team]
        each(
            team - 1,
            lambda i: send(slot, slot, pass_send, pass_recv.at[blk_now], team_peer(mate_at(i + 1))),
        )

    each(blocks - 1, send_far)
    pass_on(my_blk)
    each(blocks - 1, send_places)

    def pass_far(distance):
        blk_now = block_at(distance)
        wait_bytes(kv.at[0], own_recv.at[blk_now])
        pass_on(blk_now)

    def block_keys(blk_now, which):
        return join_rows(kv[pl.ds(blk_now * team, team), which])

    def make_columns(blk_now):
        columns[blk_now] = jnp.transpose(jnp.broadcast_to(places[blk_now], (rows, rows)))

    def score_block(distance, state):
        top, total, trace = state
        blk_now = block_at(distance)
        wait_bytes(kv.at[pl.ds(0, team - 1)], pass_recv.at[blk_now])
        found = contract_last(block_keys(blk_now, 0), queries) * scale
        block_products = contract_last(block_keys(blk_now, 1), grads)
        masked = jnp.where(place_row >= columns[blk_now], found, masked_score)
        updated = jnp.maximum(top, jnp.max(masked, axis=0, keepdims=True))
        weights = jnp.exp(masked - updated)
        scores[blk_now] = weights
        products[blk_now] = block_products
        tops[blk_now] = updated
        factor = jnp.exp(top - updated)
        total = total * factor + jnp.sum(weights, axis=0, keepdims=True)
        trace = trace * factor + jnp.sum(weights * block_products, axis=0, keepdims=True)
        return updated, total, trace

    def fold(body, init):
        if blocks <= 16:
            for index in range(blocks):
                init = body(index, init)
            return init
        return lax.fori_loop(0, blocks, body, init)

    loads[3].wait()
    loads[4].wait()
    queries = q_ref[...]
    grads = g_ref[...]
    nought = jnp.zeros((1, rows), jnp.float32)
    state = (jnp.full((1, rows), masked_score, jnp.float32), nought, nought)
    if blocks <= 16:
        order = [near_first(index, blocks) for index in range(blocks)]
        for distance in order[1:]:
            pass_far(distance)
        wait_bytes(places.at[pl.ds(0, blocks - 1)], place_recv)
        each(blocks, make_columns)
        for distance in order:
            state = score_block(distance, state)
    else:
        order = None
        each(blocks - 1, lambda i: pass_far(i + 1))
        wait_bytes(places.at[pl.ds(0, blocks - 1)], place_recv)
        each(blocks, make_columns)
        state = fold(score_block, state)
    top, total, trace = state
    inverse = 1.0 / total
    delta = trace * inverse

    def grad_block(distance):
        blk_now = block_at(distance)
        weights = scores[blk_now] * (inverse * jnp.exp(tops[blk_now] - top))
        rounded = weights.astype(jnp.bfloat16)
        slopes = (weights * (products[blk_now] - delta)).astype(jnp.bfloat16)
        slopes_ref[blk_now] = slopes
        key_part = jnp.dot(slopes, queries, preferred_element_type=jnp.float32) * scale
        value_part = jnp.dot(rounded, grads, preferred_element_type=jnp.float32)
        group = pl.ds(blk_now * team, team)
        parts[group, 0] = key_part.reshape(team, piece, head_dim).astype(jnp.bfloat16)
        parts[group, 1] = value_part.reshape(team, piece, head_dim).astype(jnp.bfloat16)

        def send_part(step):
            slot = blk_now * team + 2 * half_at(step + 1) + 1 - side
            send(
                parts.at[slot],
                staged.at[slot],
                stage_send,
                stage_recv.at[blk_now],
                team_peer(twin),
            )

        each(half, send_part)

    def pair_sum(blk_now, half_now):
        slot = blk_now * team + 2 * half_now + side
        return parts[slot].astype(jnp.float32) + staged[slot].astype(jnp.float32)

    def send_sums(distance, steps):
        blk_now = block_at(distance)
        wait_bytes(staged.at[pl.ds(0, half)], stage_recv.at[blk_now])
        for step in steps:
            half_now = half_at(step)
            slot = blk_now * half + half_now
            sums_ref[slot] = pair_sum(blk_now, half_now).astype(jnp.bfloat16)
            send(
                sums_ref.at[slot],
                landed.at[my_blk * half + my_half],
                part_send,
                part_recv,
                {"blk": blk_now, "team": 2 * half_now + side},
            )

    def add_query(blk_now, query_sum):
        return query_sum + contract_first(slopes_ref[blk_now], block_keys(blk_now, 0))

    if order:
        for distance in order[::-1]:
            grad_block(distance)
    else:
        each(blocks, lambda i: grad_block(i))
    query_sum = fold(add_query, jnp.zeros((rows, head_dim), jnp.float32))
    qg_ref[...] = (query_sum * scale).astype(jnp.bfloat16)
    every = list(range(half))[::-1]
    if order:
        for distance in order[:0:-1]:
            send_sums(distance, every)
    else:
        each(blocks - 1, lambda i: send_sums(i + 1, every))
    send_sums(0, every[:-1])
    sums = pair_sum(my_blk, my_half)
    wait_bytes(kv.at[pl.ds(0, blocks - 1)], own_send)
    wait_bytes(kv.at[pl.ds(0, blocks * (team - 1))], pass_send)
    wait_bytes(places.at[pl.ds(0, blocks - 1)], place_send)
    wait_bytes(staged.at[pl.ds(0, blocks * half)], stage_send)
    wait_bytes(landed.at[pl.ds(0, blocks * half - 1)], part_recv)

    def add_landed(index, sums):
        away = jnp.int32(index + 1)
        blk_now = block_at(lax.div(away, jnp.int32(half)))
        slot = blk_now * half + half_at(lax.rem(away, jnp.int32(half)))
        return sums + landed[slot].astype(jnp.float32)

    if blocks * half <= 16:
        for index in range(blocks * half - 1):
            sums = add_landed(index, sums)
    else:
        sums = lax.fori_loop(0, blocks * half - 1, add_landed, sums)
    kg_ref[...] = sums[0].astype(jnp.bfloat16)
    vg_ref[...] = sums[1].astype(jnp.bfloat16)
    wait_bytes(sums_ref.at[pl.ds(0, blocks * half - 1)], part_send)


def put_out(*refs):
    count = (len(refs) - 1) // 2
    copies = [
        pltpu.make_async_copy(refs[i], refs[count + i], refs[-1].at[i]) for i in range(count)
    ]
    for copy in copies:
        copy.start()
    for copy in copies:
        copy.wait()


def per_device(queries, keys, values, out_grads, positions):
    blocks, team = lax.axis_size("blk"), lax.axis_size("team")
    n = blocks * team
    rows, head_dim = queries.shape
    piece = keys.shape[0]
    any_space = pl.BlockSpec(memory_space=pl.ANY)
    near_space = pl.BlockSpec(memory_space=pltpu.VMEM)
    results = (queries, keys, values)
    sends = pltpu.SemaphoreType.DMA
    many = pltpu.SemaphoreType.DMA((blocks,))
    slots = pltpu.VMEM((n, 2, piece, head_dim), jnp.bfloat16)
    few = pltpu.VMEM((blocks * team // 2, 2, piece, head_dim), jnp.bfloat16)
    square = pltpu.VMEM((blocks, rows, rows), jnp.float32)
    held = pl.pallas_call(
        functools.partial(kernel, blocks, team),
        out_shape=tuple(pltpu.VMEM(one.shape, jnp.bfloat16) for one in results),
        in_specs=[any_space] * 5,
        out_specs=(near_space,) * 3,
        scratch_shapes=[
            pltpu.VMEM((rows, head_dim), jnp.bfloat16),
            pltpu.VMEM((rows, head_dim), jnp.bfloat16),
            pltpu.VMEM((1, rows), jnp.int32),
            slots,
            pltpu.VMEM((blocks, 1, rows), jnp.float32),
            square,
            square,
            pltpu.VMEM((blocks, rows, rows), jnp.bfloat16),
            square,
            pltpu.VMEM((blocks, 1, rows), jnp.float32),
            slots,
            slots,
            few,
            few,
            pltpu.SemaphoreType.DMA((5,)),
            sends,
            many,
            sends,
            many,
            sends,
            sends,
            sends,
            many,
            sends,
            sends,
        ],
        compiler_params=pltpu.CompilerParams(collective_id=0, has_side_effects=True),
    )(queries, keys, values, out_grads, positions.reshape(1, rows))
    return pl.pallas_call(
        put_out,
        out_shape=tuple(jax.ShapeDtypeStruct(one.shape, jnp.bfloat16) for one in results),
        in_specs=[near_space] * 3,
        out_specs=(any_space,) * 3,
        scratch_shapes=[pltpu.SemaphoreType.DMA((3,))],
    )(*(pltpu.with_memory_space_constraint(one, pltpu.VMEM) for one in held))


def solution(mesh):
    in_specs = (
        P("blk", ("team", "heads")),
        P(("blk", "team"), "heads"),
        P(("blk", "team"), "heads"),
        P("blk", ("team", "heads")),
        P("blk"),
    )
    out_specs = (
        P("blk", ("team", "heads")),
        P(("blk", "team"), "heads"),
        P(("blk", "team"), "heads"),
    )
    return jax.shard_map(
        per_device, mesh=mesh, in_specs=in_specs, out_specs=out_specs, check_vma=False
    )
```

profile of v0, /device:TPU:0, one launch (start us, length us, event | category | flops | bytes accessed | tf_op | source)
XLA Modules:
  0.0 21.4 jit_solution(14750963667381536718)
XLA Ops:
  0.6 20.1 %shard_map.76 = (bf16[128,128]{1,0:T(8,128)(2,1)S(1)}, bf16[32,128]{1,0:T(8,128)(2,1)S(1)}, bf16[32,128]{1,0:T(8,128)(2,1)S(1)}) custom-call(bf16[128,128]{1,0:T(8,128)(2,1)} %q_hbm.1, bf16[32,128]{1,0:T(8,128)(2,1)} %k_hbm.1, bf16[32,128]{1,0:T(8,128)(2,1)} %v_hbm.1, bf16[128,128]{1,0:T(8,128)(2,1)} %g_hbm.1, s32[1,128]{1,0:T(1,128)} %bitcast.1), custom_call_target="tpu_custom_call" | custom-call | tf_op jit(solution)/shard_map/pallas_call | solution.py:343
  20.8 0.6 %shard_map.77 = (bf16[128,128]{1,0:T(8,128)(2,1)}, bf16[32,128]{1,0:T(8,128)(2,1)}, bf16[32,128]{1,0:T(8,128)(2,1)}) custom-call(bf16[128,128]{1,0:T(8,128)(2,1)S(1)} %get-tuple-element.6.refs_0_, bf16[32,128]{1,0:T(8,128)(2,1)S(1)} %get-tuple-element.7.refs_1_, bf16[32,128]{1,0:T(8,128)(2,1)S(1)} %get-tuple-element.8.refs_2_), custom_call_target="tpu_custom_call" | custom-call | tf_op jit(solution)/shard_map/pallas_call | solution.py:377
where the time goes:
time: 21.6 us; the launch traced here: 21.4 us
  Pallas kernels  20.8 us (96%)
  between operations  0.64 us (3%)
    pallas_call x1, Pallas kernels, per_device(): pl.pallas_call(functools.partial(kernel, blocks, team), out_shape=tuple((...  20.1 us
    pallas_call x1, Pallas kernels, per_device(): pl.pallas_call(put_out, out_shape=tuple((jax.ShapeDtypeStruct(one.shape,...  0.65 us

commit v1 on v0

v1 whole, which is shorter than its diff:
```python
import functools
import math

import jax
import jax.numpy as jnp
from jax import lax
from jax.experimental import pallas as pl
from jax.experimental.pallas import tpu as pltpu
from jax.sharding import PartitionSpec as P

masked_score = -1e30
MESH = pl.DeviceIdType.MESH


def contract_last(left, right):
    return lax.dot_general(
        left, right, (((1,), (1,)), ((), ())), preferred_element_type=jnp.float32
    )


def contract_first(left, right):
    return lax.dot_general(
        left, right, (((0,), (0,)), ((), ())), preferred_element_type=jnp.float32
    )


def each(count, body):
    if count <= 16:
        for index in range(count):
            body(index)
    else:

        def step(index, carry):
            body(index)
            return carry

        lax.fori_loop(0, count, step, 0)


def fold(count, body, init):
    if count <= 16:
        for index in range(count):
            init = body(index, init)
        return init
    return lax.fori_loop(0, count, body, init)


def join_rows(pieces):
    count, rows, width = pieces.shape
    if rows % 16:
        return pieces.astype(jnp.float32).reshape(count * rows, width).astype(pieces.dtype)
    return pieces.reshape(count * rows, width)


def kernel(
    blocks,
    team,
    q_hbm,
    k_hbm,
    v_hbm,
    g_hbm,
    p_hbm,
    qg_ref,
    kg_ref,
    vg_ref,
    q_ref,
    g_ref,
    p_ref,
    own,
    kv,
    start,
    starts,
    scores,
    products,
    slopes_ref,
    tops,
    stats,
    stats_in,
    query_sums,
    query_in,
    parts,
    landed,
    load_sem,
    own_send,
    own_recv,
    start_send,
    start_recv,
    head_send,
    head_recv,
    stat_send,
    stat_recv,
    part_send,
    part_recv,
    query_send,
    query_recv,
):
    my_blk, my_team = lax.axis_index("blk"), lax.axis_index("team")
    rows, head_dim = q_ref.shape[1:]
    piece = k_hbm.shape[0]
    scale = 1.0 / math.sqrt(head_dim)
    half = team // 2
    count = blocks * half
    side = lax.rem(my_team, 2)
    other = 1 - side
    my_slot = my_blk * half + lax.div(my_team, 2)
    twin = {"blk": my_blk, "team": my_team + 1 - 2 * side}

    def peer_at(slot):
        slot = jnp.int32(slot)
        return {
            "blk": lax.div(slot, jnp.int32(half)),
            "team": 2 * lax.rem(slot, jnp.int32(half)) + other,
        }

    def send(src, dst, send_sem, recv_sem, peer):
        pltpu.make_async_remote_copy(
            src_ref=src,
            dst_ref=dst,
            send_sem=send_sem,
            recv_sem=recv_sem,
            device_id=peer,
            device_id_type=MESH,
        ).start()

    def wait_bytes(ref, sem):
        pltpu.make_async_copy(ref, ref, sem).wait()

    barrier = pltpu.get_barrier_semaphore()
    each(
        count,
        lambda slot: pl.semaphore_signal(
            barrier, inc=1, device_id=peer_at(slot), device_id_type=MESH
        ),
    )

    loads = [
        pltpu.make_async_copy(k_hbm, own.at[0], load_sem.at[0]),
        pltpu.make_async_copy(v_hbm, own.at[1], load_sem.at[1]),
        pltpu.make_async_copy(p_hbm, p_ref, load_sem.at[2]),
        pltpu.make_async_copy(q_hbm, q_ref.at[side], load_sem.at[3]),
        pltpu.make_async_copy(g_hbm, g_ref.at[side], load_sem.at[4]),
    ]
    for load in loads:
        load.start()
    loads[2].wait()
    place = p_ref[...].astype(jnp.float32)
    lane = lax.broadcasted_iota(jnp.int32, (1, rows), 1)
    first = jnp.sum(jnp.where(lane == my_team * piece, place, 0.0), axis=1, keepdims=True)
    start[...] = jnp.broadcast_to(first, (1, 2 * rows))
    place_row = jnp.concatenate([place, place], axis=1)
    for which in (0, 1, 3, 4):
        loads[which].wait()
    pl.semaphore_wait(barrier, count)

    def send_own(index):
        peer = peer_at(count - 1 - index)
        send(own, kv.at[my_slot], own_send, own_recv.at[my_blk], peer)

    def send_start(index):
        peer = peer_at(count - 1 - index)
        send(start, starts.at[my_slot], start_send, start_recv, peer)

    each(count, send_own)
    send(q_ref.at[side], q_ref.at[side], head_send, head_recv, twin)
    send(g_ref.at[side], g_ref.at[side], head_send, head_recv, twin)
    each(count, send_start)

    def group(blk_now):
        return pl.ds(blk_now * half, half)

    def block_keys(blk_now, which):
        return join_rows(kv[group(blk_now), which])

    wait_bytes(q_ref, head_recv)
    wait_bytes(starts, start_recv)
    queries = join_rows(q_ref[...])
    grads = join_rows(g_ref[...])
    depth = lax.broadcasted_iota(jnp.int32, (1, piece, 2 * rows), 1).astype(jnp.float32)

    def score_block(index, state):
        top, total, trace = state
        blk_now = blocks - 1 - index
        wait_bytes(kv.at[pl.ds(0, half)], own_recv.at[blk_now])
        found = contract_last(block_keys(blk_now, 0), queries) * scale
        block_products = contract_last(block_keys(blk_now, 1), grads)
        visible = place_row.reshape(1, 1, 2 * rows) - starts[group(blk_now)] >= depth
        masked = jnp.where(visible, found.reshape(half, piece, 2 * rows), masked_score)
        masked = masked.reshape(half * piece, 2 * rows)
        updated = jnp.maximum(top, jnp.max(masked, axis=0, keepdims=True))
        weights = jnp.exp(masked - updated)
        scores[blk_now] = weights
        products[blk_now] = block_products
        tops[blk_now] = updated
        factor = jnp.exp(top - updated)
        total = total * factor + jnp.sum(weights, axis=0, keepdims=True)
        trace = trace * factor + jnp.sum(weights * block_products, axis=0, keepdims=True)
        return updated, total, trace

    nought = jnp.zeros((1, 2 * rows), jnp.float32)
    state = (jnp.full((1, 2 * rows), masked_score, jnp.float32), nought, nought)
    near_top, near_total, near_trace = fold(blocks, score_block, state)
    stats[0], stats[1], stats[2] = near_top, near_total, near_trace
    send(stats, stats_in, stat_send, stat_recv, twin)
    wait_bytes(stats_in, stat_recv)
    far_top, far_total, far_trace = stats_in[0], stats_in[1], stats_in[2]
    top = jnp.maximum(near_top, far_top)
    near_factor, far_factor = jnp.exp(near_top - top), jnp.exp(far_top - top)
    inverse = 1.0 / (near_total * near_factor + far_total * far_factor)
    delta = (near_trace * near_factor + far_trace * far_factor) * inverse

    def grad_block(blk_now):
        weights = scores[blk_now] * (inverse * jnp.exp(tops[blk_now] - top))
        rounded = weights.astype(jnp.bfloat16)
        slopes = (weights * (products[blk_now] - delta)).astype(jnp.bfloat16)
        slopes_ref[blk_now] = slopes
        key_part = jnp.dot(slopes, queries, preferred_element_type=jnp.float32) * scale
        value_part = jnp.dot(rounded, grads, preferred_element_type=jnp.float32)
        slots = group(blk_now)
        parts[slots, 0] = key_part.reshape(half, piece, head_dim).astype(jnp.bfloat16)
        parts[slots, 1] = value_part.reshape(half, piece, head_dim).astype(jnp.bfloat16)

        def send_part(index):
            slot = blk_now * half + index
            send(
                parts.at[slot],
                landed.at[my_slot],
                part_send,
                part_recv.at[my_blk],
                peer_at(slot),
            )

        each(half, send_part)

    each(blocks, grad_block)

    def add_query(blk_now, query_sum):
        return query_sum + contract_first(slopes_ref[blk_now], block_keys(blk_now, 0))

    query_sum = fold(blocks, add_query, jnp.zeros((2 * rows, head_dim), jnp.float32))
    query_sums[...] = query_sum.reshape(2, rows, head_dim)
    send(query_sums.at[other], query_in, query_send, query_recv, twin)
    wait_bytes(q_ref, head_send)
    wait_bytes(kv, own_send)
    wait_bytes(starts, start_send)
    wait_bytes(stats, stat_send)
    wait_bytes(query_in, query_recv)
    qg_ref[...] = ((query_sums[side] + query_in[...]) * scale).astype(jnp.bfloat16)

    def add_landed(blk_now, sums):
        wait_bytes(landed.at[pl.ds(0, half)], part_recv.at[blk_now])

        def add_one(index, sums):
            return sums + landed[blk_now * half + index].astype(jnp.float32)

        return fold(half, add_one, sums)

    sums = fold(blocks, add_landed, jnp.zeros((2, piece, head_dim), jnp.float32))
    kg_ref[...] = sums[0].astype(jnp.bfloat16)
    vg_ref[...] = sums[1].astype(jnp.bfloat16)
    wait_bytes(query_in, query_send)
    wait_bytes(parts, part_send)


def put_out(*refs):
    count = (len(refs) - 1) // 2
    copies = [
        pltpu.make_async_copy(refs[i], refs[count + i], refs[-1].at[i]) for i in range(count)
    ]
    for copy in copies:
        copy.start()
    for copy in copies:
        copy.wait()


def per_device(queries, keys, values, out_grads, positions):
    blocks, team = lax.axis_size("blk"), lax.axis_size("team")
    half = team // 2
    count = blocks * half
    rows, head_dim = queries.shape
    piece = keys.shape[0]
    any_space = pl.BlockSpec(memory_space=pl.ANY)
    near_space = pl.BlockSpec(memory_space=pltpu.VMEM)
    results = (queries, keys, values)
    one = pltpu.SemaphoreType.DMA
    many = pltpu.SemaphoreType.DMA((blocks,))
    heads = pltpu.VMEM((2, rows, head_dim), jnp.bfloat16)
    slots = pltpu.VMEM((count, 2, piece, head_dim), jnp.bfloat16)
    square = pltpu.VMEM((blocks, half * piece, 2 * rows), jnp.float32)
    held = pl.pallas_call(
        functools.partial(kernel, blocks, team),
        out_shape=tuple(pltpu.VMEM(one.shape, jnp.bfloat16) for one in results),
        in_specs=[any_space] * 5,
        out_specs=(near_space,) * 3,
        scratch_shapes=[
            heads,
            heads,
            pltpu.VMEM((1, rows), jnp.int32),
            pltpu.VMEM((2, piece, head_dim), jnp.bfloat16),
            slots,
            pltpu.VMEM((1, 2 * rows), jnp.float32),
            pltpu.VMEM((count, 1, 2 * rows), jnp.float32),
            square,
            square,
            pltpu.VMEM((blocks, half * piece, 2 * rows), jnp.bfloat16),
            pltpu.VMEM((blocks, 1, 2 * rows), jnp.float32),
            pltpu.VMEM((3, 1, 2 * rows), jnp.float32),
            pltpu.VMEM((3, 1, 2 * rows), jnp.float32),
            pltpu.VMEM((2, rows, head_dim), jnp.float32),
            pltpu.VMEM((rows, head_dim), jnp.float32),
            slots,
            slots,
            pltpu.SemaphoreType.DMA((5,)),
            one,
            many,
            one,
            one,
            one,
            one,
            one,
            one,
            one,
            many,
            one,
            one,
        ],
        compiler_params=pltpu.CompilerParams(collective_id=0, has_side_effects=True),
    )(queries, keys, values, out_grads, positions.reshape(1, rows))
    return pl.pallas_call(
        put_out,
        out_shape=tuple(jax.ShapeDtypeStruct(one.shape, jnp.bfloat16) for one in results),
        in_specs=[near_space] * 3,
        out_specs=(any_space,) * 3,
        scratch_shapes=[pltpu.SemaphoreType.DMA((3,))],
    )(*(pltpu.with_memory_space_constraint(one, pltpu.VMEM) for one in held))


def solution(mesh):
    in_specs = (
        P("blk", ("team", "heads")),
        P(("blk", "team"), "heads"),
        P(("blk", "team"), "heads"),
        P("blk", ("team", "heads")),
        P("blk"),
    )
    out_specs = (
        P("blk", ("team", "heads")),
        P(("blk", "team"), "heads"),
        P(("blk", "team"), "heads"),
    )
    return jax.shard_map(
        per_device, mesh=mesh, in_specs=in_specs, out_specs=out_specs, check_vma=False
    )
```

time: 21.6 us -> 18.9 us (0.87)
  Pallas kernels: 20.8 us -> 18.1 us
    pallas_call x1, Pallas kernels: 20.1 us -> 17.4 us  [per_device(): pl.pallas_call(functools.partial(kernel, blocks, team), out_shape=tuple((...]
where the time goes in v1:
time: 18.9 us; the launch traced here: 18.7 us
  Pallas kernels  18.1 us (96%)
  between operations  0.64 us (3%)
    pallas_call x1, Pallas kernels, per_device(): pl.pallas_call(functools.partial(kernel, blocks, team), out_shape=tuple((...  17.4 us
    pallas_call x1, Pallas kernels, per_device(): pl.pallas_call(put_out, out_shape=tuple((jax.ShapeDtypeStruct(one.shape,...  0.65 us

profile of v1, /device:TPU:0, one launch (start us, length us, event | category | flops | bytes accessed | tf_op | source)
XLA Modules:
  0.0 18.7 jit_solution(5689205983395795434)
XLA Ops:
  0.6 17.4 %shard_map.76 = (bf16[128,128]{1,0:T(8,128)(2,1)S(1)}, bf16[32,128]{1,0:T(8,128)(2,1)S(1)}, bf16[32,128]{1,0:T(8,128)(2,1)S(1)}) custom-call(bf16[128,128]{1,0:T(8,128)(2,1)} %q_hbm.1, bf16[32,128]{1,0:T(8,128)(2,1)} %k_hbm.1, bf16[32,128]{1,0:T(8,128)(2,1)} %v_hbm.1, bf16[128,128]{1,0:T(8,128)(2,1)} %g_hbm.1, s32[1,128]{1,0:T(1,128)} %bitcast.1), custom_call_target="tpu_custom_call" | custom-call | tf_op jit(solution)/shard_map/pallas_call | solution.py:289
  18.1 0.6 %shard_map.77 = (bf16[128,128]{1,0:T(8,128)(2,1)}, bf16[32,128]{1,0:T(8,128)(2,1)}, bf16[32,128]{1,0:T(8,128)(2,1)}) custom-call(bf16[128,128]{1,0:T(8,128)(2,1)S(1)} %get-tuple-element.6.refs_0_, bf16[32,128]{1,0:T(8,128)(2,1)S(1)} %get-tuple-element.7.refs_1_, bf16[32,128]{1,0:T(8,128)(2,1)S(1)} %get-tuple-element.8.refs_2_), custom_call_target="tpu_custom_call" | custom-call | tf_op jit(solution)/shard_map/pallas_call | solution.py:328
